TPU v7x, 32 devices: a whole 2x2x4 slice. The times are simulated.
32 devices in a mesh: replica: 4 (over z), tp: 8 (over y, x, core).
Axes of the slice: x: 2, y: 2, z: 4, core: 2. Of those that a mesh axis runs over, the one named last changes fastest.
Arguments:
- hidden: bfloat16 [256, 8192], P(('replica', 'tp')), may hold values from -64 to 64
- head: bfloat16 [152064, 8192], P(('replica', 'tp'))
- token_ids: int32 [256], replicated, may hold values from 0 to 152063
Outputs:
- logprob: float32 [256], P(('replica', 'tp'))
All inputs are finite; a program needn't handle non-finite values.
Results may differ from a plain program's by a relative error of at most 0.0003.
Values may be sent and summed in bfloat16 or wider, within the bound.
A program may use at most 128 MiB of HBM per device.

v0:
```python
import jax
import jax.numpy as jnp
from jax import lax
from jax.sharding import PartitionSpec as P


def shards(hidden, head, token_ids):
    device_count = lax.axis_size("replica") * lax.axis_size("tp")
    per_device = hidden.shape[0]
    local_vocab = head.shape[0]
    position = lax.axis_index(("replica", "tp"))
    columns = position * local_vocab + jnp.arange(local_vocab, dtype=jnp.int32)
    gathered = lax.all_gather(hidden, ("replica", "tp"), axis=0, tiled=True)
    logits = lax.dot_general(
        gathered, head, (((1,), (1,)), ((), ())), preferred_element_type=jnp.float32
    )
    row_top = jnp.max(logits, axis=1)
    row_total = jnp.sum(jnp.exp(logits - row_top[:, None]), axis=1)
    row_picked = jnp.sum(jnp.where(columns[None, :] == token_ids[:, None], logits, 0.0), axis=1)
    stats = (row_top, row_total, row_picked)
    row_top, row_total, row_picked = stats
    shaped = (
        row_top.reshape(device_count, per_device),
        row_total.reshape(device_count, per_device),
        row_picked.reshape(device_count, per_device),
    )
    arrived = (
        lax.all_to_all(shaped[0], ("replica", "tp"), split_axis=0, concat_axis=0, tiled=True),
        lax.all_to_all(shaped[1], ("replica", "tp"), split_axis=0, concat_axis=0, tiled=True),
        lax.all_to_all(shaped[2], ("replica", "tp"), split_axis=0, concat_axis=0, tiled=True),
    )
    final_top = jnp.max(arrived[0], axis=0)
    final_total = jnp.sum(arrived[1] * jnp.exp(arrived[0] - final_top[None, :]), axis=0)
    final_picked = jnp.sum(arrived[2], axis=0)
    return final_picked - final_top - jnp.log(final_total)


def solution(mesh):
    in_specs = (P(("replica", "tp"), None), P(("replica", "tp"), None), P())
    out_specs = P(("replica", "tp"))
    return jax.shard_map(shards, mesh=mesh, in_specs=in_specs, out_specs=out_specs, check_vma=False)
```

profile of v0, /device:TPU:0, one launch (start us, length us, event | category | flops | bytes accessed | tf_op | source)
XLA Modules:
  0.0 146.2 jit_solution(7988030538817095933)
XLA Ops:
  6.5 0.0 all-gather.2.cloned.1.call-start
  6.5 0.7 all-gather.2.cloned.1.call-update
  7.3 0.0 copy-start
  7.3 67.4 %all-gather.2.cloned.1.call-done = bf16[256,8192]{1,0:T(8,128)(2,1)} async-done(((bf16[8,8192]{1,0:T(8,128)(2,1)}), bf16[256,8192]{1,0:T(8,128)(2,1)}) %all-gather.2.cloned.1.call-update) | async-done | bytes 4194320 | tf_op jit(solution)/shard_map/all_gather | solution.py:13
  74.7 32.4 %fusion = (f32[256]{0:T(256)S(1)}, f32[256,4752]{0,1:T(8,128)}) fusion(bf16[256,8192]{1,0:T(8,128)(2,1)} %all-gather.2.cloned.1.call-done, bf16[4752,8192]{1,0:T(8,128)(2,1)} %param.4), kind=kOutput, calls=%fused_computation.5 | convolution fusion | flops 19932549120 | bytes 86918144 | tf_op jit(solution)/shard_map/dot_general | solution.py:14
  107.0 0.7 all_to_all.24
  107.7 3.4 %all-to-all-start.1 = ((f32[32,1,8]{2,1,0:T(1,128)}), f32[32,1,8]{2,1,0:T(1,128)S(1)}, u32[]{:S(2)}, u32[]{:S(2)}) async-start(f32[32,1,8]{2,1,0:T(1,128)} %bitcast.1), calls=%async_computation.1 | async-start | bytes 32768 | tf_op jit(solution)/shard_map/all_to_all | solution.py:28
  111.1 0.0 copy-done
  111.1 4.3 %select_reduce_fusion = (f32[256]{0:T(256)S(1)}, f32[256]{0:T(256)S(1)}) fusion(f32[256,4752]{0,1:T(8,128)} %get-tuple-element.8, s32[256]{0:T(256)S(1)} %copy-done, s32[4752]{0:T(1024)S(1)} %iota_add_fusion, f32[256]{0:T(256)S(1)} %get-tuple-element.7), kind=kLoop, calls=%fused_computation.1 | loop fusion | flops 6082048 | bytes 4889152 | tf_op jit(solution)/shard_map/reduce_sum | solution.py:19
  115.4 0.7 all_to_all.26
  116.1 2.2 %all-to-all-done.1 = f32[32,1,8]{2,1,0:T(1,128)S(1)} async-done(((f32[32,1,8]{2,1,0:T(1,128)}), f32[32,1,8]{2,1,0:T(1,128)S(1)}, u32[]{:S(2)}, u32[]{:S(2)}) %all-to-all-start.1) | async-done | bytes 1056 | tf_op jit(solution)/shard_map/all_to_all | solution.py:28
  118.3 3.6 %all-to-all-start.2 = ((f32[32,1,8]{2,1,0:T(1,128)}), f32[32,1,8]{2,1,0:T(1,128)S(1)}, u32[]{:S(2)}, u32[]{:S(2)}) async-start(f32[32,1,8]{2,1,0:T(1,128)} %bitcast.2), calls=%async_computation.2 | async-start | bytes 32768 | tf_op jit(solution)/shard_map/all_to_all | solution.py:29
  121.9 0.7 all_to_all.22
  122.6 0.1 reduce_max.19
  122.7 6.4 %all-to-all-done.2 = f32[32,1,8]{2,1,0:T(1,128)S(1)} async-done(((f32[32,1,8]{2,1,0:T(1,128)}), f32[32,1,8]{2,1,0:T(1,128)S(1)}, u32[]{:S(2)}, u32[]{:S(2)}) %all-to-all-start.2) | async-done | bytes 1056 | tf_op jit(solution)/shard_map/all_to_all | solution.py:29
  129.1 2.5 %all-to-all-start = ((f32[32,1,8]{2,1,0:T(1,128)}), f32[32,1,8]{2,1,0:T(1,128)S(1)}, u32[]{:S(2)}, u32[]{:S(2)}) async-start(f32[32,1,8]{2,1,0:T(1,128)} %bitcast), calls=%async_computation | async-start | bytes 32768 | tf_op jit(solution)/shard_map/all_to_all | solution.py:30
  131.6 7.1 %all-to-all-done = f32[32,1,8]{2,1,0:T(1,128)S(1)} async-done(((f32[32,1,8]{2,1,0:T(1,128)}), f32[32,1,8]{2,1,0:T(1,128)S(1)}, u32[]{:S(2)}, u32[]{:S(2)}) %all-to-all-start) | async-done | bytes 1056 | tf_op jit(solution)/shard_map/all_to_all | solution.py:30
  138.8 0.1 reduce_sum.37
  138.8 0.5 log_subtract_fusion
  (2 shorter events, 0.0 us)
Async XLA Ops:
  6.5 68.1 %all-gather.2.cloned.1.call-start = ((), (), s32[]{:S(2)}) async-start(), calls=%async_computation.3 | async-start | bytes 4325376 | tf_op jit(solution)/shard_map/all_gather | solution.py:13
  7.3 103.8 %copy-start = (s32[256]{0:T(256)S(1)}, s32[256]{0:T(256)}, u32[]{:S(2)}) copy-start(s32[256]{0:T(256)} %param.5) | copy-start | bytes 3076
  107.7 10.6 %all-to-all-start.1 = ((f32[32,1,8]{2,1,0:T(1,128)}), f32[32,1,8]{2,1,0:T(1,128)S(1)}, u32[]{:S(2)}, u32[]{:S(2)}) async-start(f32[32,1,8]{2,1,0:T(1,128)} %bitcast.1), calls=%async_computation.1 | async-start | bytes 32768 | tf_op jit(solution)/shard_map/all_to_all | solution.py:28
  118.3 10.8 %all-to-all-start.2 = ((f32[32,1,8]{2,1,0:T(1,128)}), f32[32,1,8]{2,1,0:T(1,128)S(1)}, u32[]{:S(2)}, u32[]{:S(2)}) async-start(f32[32,1,8]{2,1,0:T(1,128)} %bitcast.2), calls=%async_computation.2 | async-start | bytes 32768 | tf_op jit(solution)/shard_map/all_to_all | solution.py:29
  129.1 9.7 %all-to-all-start = ((f32[32,1,8]{2,1,0:T(1,128)}), f32[32,1,8]{2,1,0:T(1,128)S(1)}, u32[]{:S(2)}, u32[]{:S(2)}) async-start(f32[32,1,8]{2,1,0:T(1,128)} %bitcast), calls=%async_computation | async-start | bytes 32768 | tf_op jit(solution)/shard_map/all_to_all | solution.py:30
Sparse Core Ops, SparseCore 0:
  10.2 64.4 all-gather.1
where the time goes:
time: 147 us; the launch traced here: 146 us
  waiting for transfers between devices  83.9 us (57%)
  matrix products  32.4 us (22%)
  between operations  13.4 us (9%)
  starting transfers between devices  9.48 us (6%)
  other arithmetic  4.92 us (3%)
  local copies, waits for them, and re-layouts  2.07 us (1%)
    all_gather x1, waiting for transfers between devices, shards(): gathered = lax.all_gather(hidden, ('replica', 'tp'), axis=0, tiled=True)  67.4 us
    dot_general x1, matrix products, shards(): lax.dot_general(gathered, head, (((1,), (1,)), ((), ())), preferred_eleme...  32.4 us
    all_to_all x1, waiting for transfers between devices, shards(): lax.all_to_all(shaped[2], ('replica', 'tp'), split_axis=0, concat_axis=0,...  7.15 us
    all_to_all x1, waiting for transfers between devices, shards(): lax.all_to_all(shaped[1], ('replica', 'tp'), split_axis=0, concat_axis=0,...  6.43 us
    reduce_sum x1, other arithmetic, shards(): jnp.sum(jnp.where(columns[None, :] == token_ids[:, None], logits, 0.0), a...  4.26 us
    all_to_all x1, starting transfers between devices, shards(): lax.all_to_all(shaped[1], ('replica', 'tp'), split_axis=0, concat_axis=0,...  3.62 us
    all_to_all x1, starting transfers between devices, shards(): lax.all_to_all(shaped[0], ('replica', 'tp'), split_axis=0, concat_axis=0,...  3.38 us
  transfers between devices with their start and end apart: 4, of which 4 were waited for; matrix products, arithmetic and copies ran while one was open for 3% of the time, Pallas kernels for 0%

commit v1 on v0

--- a/solution.py
+++ b/solution.py
@@ -10,7 +10,12 @@
     local_vocab = head.shape[0]
     position = lax.axis_index(("replica", "tp"))
     columns = position * local_vocab + jnp.arange(local_vocab, dtype=jnp.int32)
-    gathered = lax.all_gather(hidden, ("replica", "tp"), axis=0, tiled=True)
+    gathered = jnp.concatenate(
+        lax.all_to_all(
+            jnp.stack([hidden] * lax.axis_size(("replica", "tp"))), ("replica", "tp"), 0, 0
+        ),
+        axis=0,
+    )
     logits = lax.dot_general(
         gathered, head, (((1,), (1,)), ((), ())), preferred_element_type=jnp.float32
     )

time: 147 us -> 170 us (1.16)
  waiting for transfers between devices: 83.9 us -> 109 us
  between operations: 13.4 us -> 0.07 us
  starting transfers between devices: 9.48 us -> 17.7 us
  local copies, waits for them, and re-layouts: 2.07 us -> 5.37 us
    all_to_all x0 -> x1, waiting for transfers between devices: none -> 93.7 us  [shards(): lax.all_to_all(jnp.stack([hidden] * lax.axis_size(('replica', 'tp'))), ('...]
    all_gather x1 -> x0, waiting for transfers between devices: 67.4 us -> none  [shards(): gathered = lax.all_gather(hidden, ('replica', 'tp'), axis=0, tiled=True)]
    all_to_all x0 -> x1, starting transfers between devices: none -> 7.45 us  [shards(): lax.all_to_all(jnp.stack([hidden] * lax.axis_size(('replica', 'tp'))), ('...]
    another operation x0 -> x1, local copies, waits for them, and re-layouts: none -> 3.3 us  [shards(): jnp.stack([hidden] * lax.axis_size(('replica', 'tp')))]
where the time goes in v1:
time: 170 us
  waiting for transfers between devices  109 us (64%)
  matrix products  32.4 us (19%)
  starting transfers between devices  17.7 us (10%)
  local copies, waits for them, and re-layouts  5.37 us (3%)
  other arithmetic  4.91 us (3%)
    all_to_all x1, waiting for transfers between devices, shards(): lax.all_to_all(jnp.stack([hidden] * lax.axis_size(('replica', 'tp'))), ('...  93.7 us
    dot_general x1, matrix products, shards(): lax.dot_general(gathered, head, (((1,), (1,)), ((), ())), preferred_eleme...  32.4 us
    all_to_all x1, starting transfers between devices, shards(): lax.all_to_all(jnp.stack([hidden] * lax.axis_size(('replica', 'tp'))), ('...  7.45 us
    all_to_all x1, waiting for transfers between devices, shards(): lax.all_to_all(shaped[2], ('replica', 'tp'), split_axis=0, concat_axis=0,...  7.15 us
    all_to_all x1, waiting for transfers between devices, shards(): lax.all_to_all(shaped[1], ('replica', 'tp'), split_axis=0, concat_axis=0,...  6.43 us
    reduce_sum x1, other arithmetic, shards(): jnp.sum(jnp.where(columns[None, :] == token_ids[:, None], logits, 0.0), a...  4.25 us
    all_to_all x1, starting transfers between devices, shards(): lax.all_to_all(shaped[0], ('replica', 'tp'), split_axis=0, concat_axis=0,...  4.11 us
    all_to_all x1, starting transfers between devices, shards(): lax.all_to_all(shaped[1], ('replica', 'tp'), split_axis=0, concat_axis=0,...  3.61 us
  transfers between devices with their start and end apart: 4, of which 4 were waited for; matrix products, arithmetic and copies ran while one was open for 3% of the time, Pallas kernels for 0%

profile of v1, /device:TPU:0, one launch (start us, length us, event | category | flops | bytes accessed | tf_op | source)
XLA Modules:
  0.0 169.9 jit_solution(5472470360084303510)
XLA Ops:
  0.0 3.3 %stack.2 = bf16[32,8,8192]{2,1,0:T(8,128)(2,1)} broadcast(bf16[8,8192]{1,0:T(8,128)(2,1)} %param.3), dimensions={1,2} | broadcast | bytes 4325376 | tf_op jit(solution)/shard_map/stack | solution.py:15
  3.3 7.5 %all-to-all-start = ((bf16[32,8,8192]{2,1,0:T(8,128)(2,1)}), bf16[32,8,8192]{2,1,0:T(8,128)(2,1)}, u32[]{:S(2)}, u32[]{:S(2)}) async-start(bf16[32,8,8192]{2,1,0:T(8,128)(2,1)} %stack.2), calls=%async_computation | async-start | bytes 8388608 | tf_op jit(solution)/shard_map/all_to_all | solution.py:14
  10.8 0.0 copy-start
  10.8 93.7 %all-to-all-done = bf16[32,8,8192]{2,1,0:T(8,128)(2,1)} async-done(((bf16[32,8,8192]{2,1,0:T(8,128)(2,1)}), bf16[32,8,8192]{2,1,0:T(8,128)(2,1)}, u32[]{:S(2)}, u32[]{:S(2)}) %all-to-all-start) | async-done | bytes 4194336 | tf_op jit(solution)/shard_map/all_to_all | solution.py:14
  104.5 32.4 %fusion.2 = (f32[256]{0:T(256)S(1)}, f32[256,4752]{0,1:T(8,128)}) fusion(bf16[4752,8192]{1,0:T(8,128)(2,1)} %param.4, bf16[32,8,8192]{2,1,0:T(8,128)(2,1)} %all-to-all-done), kind=kOutput, calls=%fused_computation.7 | convolution fusion | flops 19932549120 | bytes 86918144 | tf_op jit(solution)/shard_map/dot_general | solution.py:19
  136.8 0.7 all_to_all.28
  137.5 4.1 %all-to-all-start.2 = ((f32[32,1,8]{2,1,0:T(1,128)}), f32[32,1,8]{2,1,0:T(1,128)S(1)}, u32[]{:S(2)}, u32[]{:S(2)}) async-start(f32[32,1,8]{2,1,0:T(1,128)} %bitcast.2), calls=%async_computation.2 | async-start | bytes 32768 | tf_op jit(solution)/shard_map/all_to_all | solution.py:33
  141.6 0.0 copy-done
  141.6 4.3 %select_reduce_fusion = (f32[256]{0:T(256)S(1)}, f32[256]{0:T(256)S(1)}) fusion(f32[256,4752]{0,1:T(8,128)} %get-tuple-element.8, s32[256]{0:T(256)S(1)} %copy-done, s32[4752]{0:T(1024)S(1)} %iota_add_fusion, f32[256]{0:T(256)S(1)} %get-tuple-element.7), kind=kLoop, calls=%fused_computation.1 | loop fusion | flops 6082048 | bytes 4889152 | tf_op jit(solution)/shard_map/reduce_sum | solution.py:24
  145.9 0.7 all_to_all.30
  146.6 2.2 %all-to-all-done.2 = f32[32,1,8]{2,1,0:T(1,128)S(1)} async-done(((f32[32,1,8]{2,1,0:T(1,128)}), f32[32,1,8]{2,1,0:T(1,128)S(1)}, u32[]{:S(2)}, u32[]{:S(2)}) %all-to-all-start.2) | async-done | bytes 1056 | tf_op jit(solution)/shard_map/all_to_all | solution.py:33
  148.8 3.6 %all-to-all-start.3 = ((f32[32,1,8]{2,1,0:T(1,128)}), f32[32,1,8]{2,1,0:T(1,128)S(1)}, u32[]{:S(2)}, u32[]{:S(2)}) async-start(f32[32,1,8]{2,1,0:T(1,128)} %bitcast.3), calls=%async_computation.3 | async-start | bytes 32768 | tf_op jit(solution)/shard_map/all_to_all | solution.py:34
  152.4 0.7 all_to_all.26
  153.1 0.1 reduce_max.19
  153.2 6.4 %all-to-all-done.3 = f32[32,1,8]{2,1,0:T(1,128)S(1)} async-done(((f32[32,1,8]{2,1,0:T(1,128)}), f32[32,1,8]{2,1,0:T(1,128)S(1)}, u32[]{:S(2)}, u32[]{:S(2)}) %all-to-all-start.3) | async-done | bytes 1056 | tf_op jit(solution)/shard_map/all_to_all | solution.py:34
  159.6 2.5 %all-to-all-start.1 = ((f32[32,1,8]{2,1,0:T(1,128)}), f32[32,1,8]{2,1,0:T(1,128)S(1)}, u32[]{:S(2)}, u32[]{:S(2)}) async-start(f32[32,1,8]{2,1,0:T(1,128)} %bitcast.1), calls=%async_computation.1 | async-start | bytes 32768 | tf_op jit(solution)/shard_map/all_to_all | solution.py:35
  162.1 7.1 %all-to-all-done.1 = f32[32,1,8]{2,1,0:T(1,128)S(1)} async-done(((f32[32,1,8]{2,1,0:T(1,128)}), f32[32,1,8]{2,1,0:T(1,128)S(1)}, u32[]{:S(2)}, u32[]{:S(2)}) %all-to-all-start.1) | async-done | bytes 1056 | tf_op jit(solution)/shard_map/all_to_all | solution.py:35
  169.3 0.1 reduce_sum.37
  169.3 0.5 log_subtract_fusion
  (2 shorter events, 0.0 us)
Async XLA Ops:
  3.3 101.2 %all-to-all-start = ((bf16[32,8,8192]{2,1,0:T(8,128)(2,1)}), bf16[32,8,8192]{2,1,0:T(8,128)(2,1)}, u32[]{:S(2)}, u32[]{:S(2)}) async-start(bf16[32,8,8192]{2,1,0:T(8,128)(2,1)} %stack.2), calls=%async_computation | async-start | bytes 8388608 | tf_op jit(solution)/shard_map/all_to_all | solution.py:14
  10.8 130.9 %copy-start = (s32[256]{0:T(256)S(1)}, s32[256]{0:T(256)}, u32[]{:S(2)}) copy-start(s32[256]{0:T(256)} %param.5) | copy-start | bytes 3076
  137.5 11.3 %all-to-all-start.2 = ((f32[32,1,8]{2,1,0:T(1,128)}), f32[32,1,8]{2,1,0:T(1,128)S(1)}, u32[]{:S(2)}, u32[]{:S(2)}) async-start(f32[32,1,8]{2,1,0:T(1,128)} %bitcast.2), calls=%async_computation.2 | async-start | bytes 32768 | tf_op jit(solution)/shard_map/all_to_all | solution.py:33
  148.8 10.8 %all-to-all-start.3 = ((f32[32,1,8]{2,1,0:T(1,128)}), f32[32,1,8]{2,1,0:T(1,128)S(1)}, u32[]{:S(2)}, u32[]{:S(2)}) async-start(f32[32,1,8]{2,1,0:T(1,128)} %bitcast.3), calls=%async_computation.3 | async-start | bytes 32768 | tf_op jit(solution)/shard_map/all_to_all | solution.py:34
  159.6 9.7 %all-to-all-start.1 = ((f32[32,1,8]{2,1,0:T(1,128)}), f32[32,1,8]{2,1,0:T(1,128)S(1)}, u32[]{:S(2)}, u32[]{:S(2)}) async-start(f32[32,1,8]{2,1,0:T(1,128)} %bitcast.1), calls=%async_computation.1 | async-start | bytes 32768 | tf_op jit(solution)/shard_map/all_to_all | solution.py:35
